TPU v7x, 32 devices: a whole 2x2x4 slice. The times are simulated.
32 devices in a mesh: trial: 4 (over x, core), north: 2 (over y), east: 4 (over z).
Axes of the slice: x: 2, y: 2, z: 4, core: 2. Of those that a mesh axis runs over, the one named last changes fastest.
Arguments:
- pair_state: bfloat16 [192, 48, 128], P(('trial', 'north'), 'east'), parts along dimension 0, may hold values from -6 to 6
- in_gain: float32 [128], replicated, may hold values from 0.25 to 1.75
- left_weight: bfloat16 [512, 128], P('trial'), parts along dimension 0, may hold values from -0.5 to 0.5
- right_weight: bfloat16 [512, 128], P('trial'), parts along dimension 0, may hold values from -0.5 to 0.5
- left_gate: bfloat16 [512, 128], P('trial'), parts along dimension 0, may hold values from -0.5 to 0.5
- right_gate: bfloat16 [512, 128], P('trial'), parts along dimension 0, may hold values from -0.5 to 0.5
- mid_gain: float32 [128], replicated, may hold values from 0.25 to 1.75
- out_weight: bfloat16 [512, 128], P('trial'), parts along dimension 0, may hold values from -0.5 to 0.5
- out_gate: bfloat16 [512, 128], P('trial'), parts along dimension 0, may hold values from -0.5 to 0.5
Outputs:
- triangle_out: bfloat16 [192, 48, 128], P(('trial', 'north'), 'east'), parts along dimension 0
There are 4 independent parts, one for each index of `trial`. A program takes and returns all parts, laid end to end along the dimension named above; an argument that names none is the same for every part. Nothing has to cross between parts.
All inputs are finite; a program needn't handle non-finite values.
Results may differ from a plain program's by a relative error of at most 0.015.
Values may be sent and summed in bfloat16 or wider, within the bound.
A program may use at most 64 MiB of HBM per device.

v0:
```python
import jax
import jax.numpy as jnp
from jax import lax
from jax.sharding import PartitionSpec as P


def norm_channels(values, channel_gain):
    centred = values - jnp.mean(values, axis=-1, keepdims=True)
    return (
        centred
        * lax.rsqrt(jnp.mean(centred * centred, axis=-1, keepdims=True) + 1e-05)
        * channel_gain
    )


def make_factors(pair_in, in_gain, left_weight, right_weight, left_gate, right_gate):
    ready = norm_channels(pair_in.astype(jnp.float32), in_gain).astype(jnp.bfloat16)
    ready = lax.optimization_barrier(ready)
    left = jnp.einsum("ijc,cd->ijd", ready, left_weight, preferred_element_type=jnp.float32)
    left = left * jax.nn.sigmoid(
        jnp.einsum("ijc,cd->ijd", ready, left_gate, preferred_element_type=jnp.float32)
    )
    right = jnp.einsum("ijc,cd->ijd", ready, right_weight, preferred_element_type=jnp.float32)
    right = right * jax.nn.sigmoid(
        jnp.einsum("ijc,cd->ijd", ready, right_gate, preferred_element_type=jnp.float32)
    )
    return (ready, left.astype(jnp.bfloat16), right.astype(jnp.bfloat16))


def to_pair(mixed, ready, mid_gain, out_weight, out_gate):
    scaled = norm_channels(mixed.astype(jnp.float32), mid_gain).astype(jnp.bfloat16)
    scaled = lax.optimization_barrier(scaled)
    gate = jax.nn.sigmoid(
        jnp.einsum("ijc,cd->ijd", ready, out_gate, preferred_element_type=jnp.float32)
    )
    return (
        jnp.einsum("ijd,dc->ijc", scaled, out_weight, preferred_element_type=jnp.float32) * gate
    ).astype(jnp.bfloat16)


def local(
    pair_state,
    in_gain,
    left_weight,
    right_weight,
    left_gate,
    right_gate,
    mid_gain,
    out_weight,
    out_gate,
):
    ready, left, right = make_factors(
        pair_state, in_gain, left_weight, right_weight, left_gate, right_gate
    )
    count = pair_state.shape[1] * lax.axis_size("east")
    left_lines, right_lines = (
        lax.all_to_all(left, "east", split_axis=2, concat_axis=1, tiled=True),
        lax.all_to_all(right, "east", split_axis=2, concat_axis=1, tiled=True),
    )
    strip = jnp.einsum(
        "ikd,jkd->ijd",
        left_lines,
        lax.all_gather(right_lines, "north", axis=0, tiled=True),
        preferred_element_type=jnp.float32,
    )
    strip = (strip * count ** (-0.5)).astype(jnp.bfloat16)
    mixed = lax.all_to_all(strip, "east", split_axis=1, concat_axis=2, tiled=True)
    return to_pair(mixed, ready, mid_gain, out_weight, out_gate)


def solution(mesh):
    return jax.shard_map(
        local,
        mesh=mesh,
        in_specs=(
            P(("trial", "north"), "east", None),
            P(),
            P("trial", None),
            P("trial", None),
            P("trial", None),
            P("trial", None),
            P(),
            P("trial", None),
            P("trial", None),
        ),
        out_specs=P(("trial", "north"), "east", None),
        check_vma=False,
    )
```

profile of v0, /device:TPU:0, one launch (start us, length us, event | category | flops | bytes accessed | tf_op | source)
XLA Modules:
  0.0 44.6 jit_solution(821063206014544712)
XLA Ops:
  0.0 1.1 %convert_reduce_fusion = f32[24,12]{0,1:T(8,128)S(1)} fusion(bf16[24,12,128]{2,0,1:T(8,128)(2,1)} %param.9), kind=kLoop, calls=%fused_computation.25 | loop fusion | flops 73440 | bytes 74880 | tf_op jit(solution)/shard_map/reduce_sum | solution.py:8
  1.3 0.6 %copy-done.4 = f32[128]{0:T(128)S(1)} copy-done((f32[128]{0:T(128)S(1)}, f32[128]{0:T(128)}, u32[]{:S(2)}) %copy-start.4) | copy-done | bytes 536
  2.3 0.6 %copy-done.6 = bf16[128,128]{1,0:T(8,128)(2,1)S(1)} copy-done((bf16[128,128]{1,0:T(8,128)(2,1)S(1)}, bf16[128,128]{1,0:T(8,128)(2,1)}, u32[]{:S(2)}) %copy-start.6) | copy-done | bytes 32792
  3.1 0.4 copy.34
  3.5 1.1 %reshape.41 = bf16[4,2,4608]{2,1,0:T(2,128)(2,1)} reshape(bf16[128,12,24]{2,1,0:T(8,128)(2,1)S(1)} %bitcast.55) | data formatting | bytes 147456
  4.7 6.5 %all-to-all-start = ((bf16[4,2,4608]{2,1,0:T(2,128)(2,1)}), bf16[4,2,4608]{2,1,0:T(2,128)(2,1)S(1)}, u32[]{:S(2)}, u32[]{:S(2)}) async-start(bf16[4,2,4608]{2,1,0:T(2,128)(2,1)} %reshape.41), calls=%async_computation | async-start | bytes 147456 | tf_op jit(solution)/shard_map/all_to_all | solution.py:58
  11.3 0.6 %copy-done.7 = bf16[128,128]{1,0:T(8,128)(2,1)S(1)} copy-done((bf16[128,128]{1,0:T(8,128)(2,1)S(1)}, bf16[128,128]{1,0:T(8,128)(2,1)}, u32[]{:S(2)}) %copy-start.7) | copy-done | bytes 32792
  12.1 0.4 copy.37
  12.5 1.1 %reshape.43 = bf16[4,2,4608]{2,1,0:T(2,128)(2,1)} reshape(bf16[128,12,24]{2,1,0:T(8,128)(2,1)S(1)} %bitcast.56) | data formatting | bytes 147456
  13.7 3.2 %all-to-all-done = bf16[4,2,4608]{2,1,0:T(2,128)(2,1)S(1)} async-done(((bf16[4,2,4608]{2,1,0:T(2,128)(2,1)}), bf16[4,2,4608]{2,1,0:T(2,128)(2,1)S(1)}, u32[]{:S(2)}, u32[]{:S(2)}) %all-to-all-start) | async-done | bytes 73760 | tf_op jit(solution)/shard_map/all_to_all | solution.py:58
  16.9 3.3 %all-to-all-start.1 = ((bf16[4,2,4608]{2,1,0:T(2,128)(2,1)}), bf16[4,2,4608]{2,1,0:T(2,128)(2,1)S(1)}, u32[]{:S(2)}, u32[]{:S(2)}) async-start(bf16[4,2,4608]{2,1,0:T(2,128)(2,1)} %reshape.43), calls=%async_computation.1 | async-start | bytes 147456 | tf_op jit(solution)/shard_map/all_to_all | solution.py:57
  20.2 0.6 %reshape.42 = bf16[128,12,24]{2,1,0:T(8,128)(2,1)S(1)} reshape(bf16[4,2,4608]{2,1,0:T(2,128)(2,1)S(1)} %all-to-all-done) | data formatting | bytes 147456
  20.8 0.4 copy.35
  21.5 6.3 %all_gather.3 = bf16[48,48,32]{1,0,2:T(8,128)(2,1)S(1)} all-gather(bf16[24,48,32]{1,0,2:T(8,128)(2,1)S(1)} %copy.36), channel_id=1, replica_groups=mesh['trial'=4,'north'=2,'east'=4] {'north'}, dimensions={0}, use_global_device_ids=true | all-gather | bytes 221184 | tf_op jit(solution)/shard_map/all_gather | solution.py:63
  27.8 0.6 %reshape.44 = bf16[128,12,24]{2,1,0:T(8,128)(2,1)S(1)} reshape(bf16[4,2,4608]{2,1,0:T(2,128)(2,1)S(1)} %all-to-all-done.1) | data formatting | bytes 147456
  28.4 0.4 copy.38
  29.1 0.3 fusion.1
  29.9 10.6 %all_to_all.45 = bf16[4,2,4608]{2,1,0:T(2,128)(2,1)S(1)} all-to-all(bf16[4,2,4608]{2,1,0:T(2,128)(2,1)S(1)} %reshape.45), channel_id=1, replica_groups=mesh['trial'=4,'north'=2,'east'=4] {'east'}, dimensions={0} | all-to-all | bytes 147456 | tf_op jit(solution)/shard_map/all_to_all | solution.py:67
  41.2 0.4 copy.41
  41.6 0.3 reshape.32
  41.9 0.4 copy-done.5
  42.4 0.6 %copy-done.3 = bf16[128,128]{1,0:T(8,128)(2,1)S(1)} copy-done((bf16[128,128]{1,0:T(8,128)(2,1)S(1)}, bf16[128,128]{1,0:T(8,128)(2,1)}, u32[]{:S(2)}) %copy-start.3) | copy-done | bytes 32792
  43.2 0.6 %copy-done.8 = bf16[128,128]{1,0:T(8,128)(2,1)S(1)} copy-done((bf16[128,128]{1,0:T(8,128)(2,1)S(1)}, bf16[128,128]{1,0:T(8,128)(2,1)}, u32[]{:S(2)}) %copy-start.8) | copy-done | bytes 32792
  43.7 0.8 %fusion.14 = bf16[24,12,128]{2,0,1:T(8,128)(2,1)} fusion(f32[24,12,128]{2,0,1:T(8,128)S(1)} %fusion.24, bf16[24,12,128]{2,0,1:T(8,128)(2,1)S(1)} %fusion.22, bf16[128,128]{1,0:T(8,128)(2,1)S(1)} %copy-done.8), kind=kOutput, calls=%fused_computation.18 | convolution fusion | flops 9621504 | bytes 327680 | tf_op jit(solution)/shard_map/ijc,cd->ijd/dot_general | solution.py:34
  (33 shorter events, 3.0 us)
Async XLA Ops:
  0.0 2.1 %copy-start = (bf16[128,128]{1,0:T(8,128)(2,1)S(1)}, bf16[128,128]{1,0:T(8,128)(2,1)}, u32[]{:S(2)}) copy-start(bf16[128,128]{1,0:T(8,128)(2,1)} %param.12) | copy-start | bytes 98308
  0.0 1.1 %copy-start.1 = (bf16[24,12,128]{2,0,1:T(8,128)(2,1)S(1)}, bf16[24,12,128]{2,0,1:T(8,128)(2,1)}, u32[]{:S(2)}) copy-start(bf16[24,12,128]{2,0,1:T(8,128)(2,1)} %param.9) | copy-start | bytes 221188
  1.3 0.7 %copy-start.4 = (f32[128]{0:T(128)S(1)}, f32[128]{0:T(128)}, u32[]{:S(2)}) copy-start(f32[128]{0:T(128)} %param.10) | copy-start | bytes 1540
  2.1 0.8 %copy-start.6 = (bf16[128,128]{1,0:T(8,128)(2,1)S(1)}, bf16[128,128]{1,0:T(8,128)(2,1)}, u32[]{:S(2)}) copy-start(bf16[128,128]{1,0:T(8,128)(2,1)} %param.14) | copy-start | bytes 98308
  4.7 6.5 %copy-start.2 = (bf16[128,128]{1,0:T(8,128)(2,1)S(1)}, bf16[128,128]{1,0:T(8,128)(2,1)}, u32[]{:S(2)}) copy-start(bf16[128,128]{1,0:T(8,128)(2,1)} %param.11) | copy-start | bytes 98308
  4.7 12.2 %all-to-all-start = ((bf16[4,2,4608]{2,1,0:T(2,128)(2,1)}), bf16[4,2,4608]{2,1,0:T(2,128)(2,1)S(1)}, u32[]{:S(2)}, u32[]{:S(2)}) async-start(bf16[4,2,4608]{2,1,0:T(2,128)(2,1)} %reshape.41), calls=%async_computation | async-start | bytes 147456 | tf_op jit(solution)/shard_map/all_to_all | solution.py:58
  11.1 0.8 %copy-start.7 = (bf16[128,128]{1,0:T(8,128)(2,1)S(1)}, bf16[128,128]{1,0:T(8,128)(2,1)}, u32[]{:S(2)}) copy-start(bf16[128,128]{1,0:T(8,128)(2,1)} %param.13) | copy-start | bytes 98308
  16.9 10.9 %all-to-all-start.1 = ((bf16[4,2,4608]{2,1,0:T(2,128)(2,1)}), bf16[4,2,4608]{2,1,0:T(2,128)(2,1)S(1)}, u32[]{:S(2)}, u32[]{:S(2)}) async-start(bf16[4,2,4608]{2,1,0:T(2,128)(2,1)} %reshape.43), calls=%async_computation.1 | async-start | bytes 147456 | tf_op jit(solution)/shard_map/all_to_all | solution.py:57
  41.6 0.7 %copy-start.5 = (f32[128]{0:T(128)S(1)}, f32[128]{0:T(128)}, u32[]{:S(2)}) copy-start(f32[128]{0:T(128)} %param.15) | copy-start | bytes 1540
  42.2 0.8 %copy-start.3 = (bf16[128,128]{1,0:T(8,128)(2,1)S(1)}, bf16[128,128]{1,0:T(8,128)(2,1)}, u32[]{:S(2)}) copy-start(bf16[128,128]{1,0:T(8,128)(2,1)} %param.16) | copy-start | bytes 98308
  43.0 0.8 %copy-start.8 = (bf16[128,128]{1,0:T(8,128)(2,1)S(1)}, bf16[128,128]{1,0:T(8,128)(2,1)}, u32[]{:S(2)}) copy-start(bf16[128,128]{1,0:T(8,128)(2,1)} %param.17) | copy-start | bytes 98308
where the time goes:
time: 45.3 us; the launch traced here: 44.6 us
  blocking collectives  17 us (38%)
  local copies, waits for them, and re-layouts  10.4 us (23%)
  starting transfers between devices  9.77 us (22%)
  waiting for transfers between devices  3.24 us (7%)
  matrix products  2.02 us (4%)
  other arithmetic  1.96 us (4%)
    all_to_all x1, blocking collectives, local(): lax.all_to_all(strip, 'east', split_axis=1, concat_axis=2, tiled=True)  10.6 us
    unnamed x24, local copies, waits for them, and re-layouts  7.31 us
    all_to_all x1, starting transfers between devices, local(): lax.all_to_all(right, 'east', split_axis=2, concat_axis=1, tiled=True)  6.48 us
    all_gather x1, blocking collectives, local(): lax.all_gather(right_lines, 'north', axis=0, tiled=True)  6.34 us
    all_to_all x1, starting transfers between devices, local(): lax.all_to_all(left, 'east', split_axis=2, concat_axis=1, tiled=True)  3.29 us
    all_to_all x1, waiting for transfers between devices, local(): lax.all_to_all(right, 'east', split_axis=2, concat_axis=1, tiled=True)  3.23 us
    reduce_sum x2, other arithmetic, norm_channels(): centred = values - jnp.mean(values, axis=-1, keepdims=True)  1.19 us
  transfers between devices with their start and end apart: 2, of which 1 were waited for; matrix products, arithmetic and copies ran while one was open for 7% of the time, Pallas kernels for 0%

commit v1 on v0

--- a/solution.py
+++ b/solution.py
@@ -57,12 +57,27 @@
         lax.all_to_all(left, "east", split_axis=2, concat_axis=1, tiled=True),
         lax.all_to_all(right, "east", split_axis=2, concat_axis=1, tiled=True),
     )
-    strip = jnp.einsum(
-        "ikd,jkd->ijd",
-        left_lines,
-        lax.all_gather(right_lines, "north", axis=0, tiled=True),
-        preferred_element_type=jnp.float32,
+    here_x = right_lines
+    local_part, current_block, row_out = (
+        lax.psum(1, "north"),
+        lax.axis_index("north"),
+        here_x.shape[0],
     )
+    runs = []
+    for c in range(local_part):
+        aux = (
+            lax.ppermute(
+                here_x, "north", [(to_i, (to_i + 1) % local_part) for to_i in range(local_part)]
+            )
+            if c + 1 < local_part
+            else here_x
+        )
+        runs.append(
+            jnp.einsum("ikd,jkd->ijd", left_lines, here_x, preferred_element_type=jnp.float32)
+        )
+        here_x = aux
+    inter = jnp.concatenate(runs[::-1], axis=1)
+    strip = jnp.roll(inter, shift=(current_block + 1) * runs[0].shape[1], axis=1)
     strip = (strip * count ** (-0.5)).astype(jnp.bfloat16)
     mixed = lax.all_to_all(strip, "east", split_axis=1, concat_axis=2, tiled=True)
     return to_pair(mixed, ready, mid_gain, out_weight, out_gate)

time: 45.3 us -> 43.8 us (0.967)
  blocking collectives: 17 us -> 10.4 us
  waiting for transfers between devices: 3.24 us -> 6.09 us
  starting transfers between devices: 9.77 us -> 11.4 us
  other arithmetic: 1.96 us -> 2.45 us
    all_gather x1 -> x0, blocking collectives: 6.34 us -> none  [local(): lax.all_gather(right_lines, 'north', axis=0, tiled=True)]
    all_to_all x1, waiting for transfers between devices: 0.01 us -> 2.86 us  [local(): lax.all_to_all(left, 'east', split_axis=2, concat_axis=1, tiled=True)]
    ppermute x0 -> x1, starting transfers between devices: none -> 1.58 us  [local(): lax.ppermute(here_x, 'north', [(to_i, (to_i + 1) % local_part) for to_i i...]
    convert_element_type x0 -> x1, other arithmetic: none -> 0.49 us  [local(): strip = (strip * count ** (-0.5)).astype(jnp.bfloat16)]
  transfers between devices with their start and end apart: 2 -> 3, of which waited for: 1 -> 2; matrix products, arithmetic and copies ran while one was open for 7% -> 11% of each run, Pallas kernels for 0% -> 0%
where the time goes in v1:
time: 43.8 us; the launch traced here: 43.1 us
  starting transfers between devices  11.4 us (26%)
  local copies, waits for them, and re-layouts  10.4 us (24%)
  blocking collectives  10.4 us (24%)
  waiting for transfers between devices  6.09 us (14%)
  other arithmetic  2.45 us (6%)
  matrix products  2.16 us (5%)
    all_to_all x1, blocking collectives, local(): lax.all_to_all(strip, 'east', split_axis=1, concat_axis=2, tiled=True)  10.4 us
    unnamed x24, local copies, waits for them, and re-layouts  7.32 us
    all_to_all x1, starting transfers between devices, local(): lax.all_to_all(right, 'east', split_axis=2, concat_axis=1, tiled=True)  6.48 us
    all_to_all x1, starting transfers between devices, local(): lax.all_to_all(left, 'east', split_axis=2, concat_axis=1, tiled=True)  3.29 us
    all_to_all x1, waiting for transfers between devices, local(): lax.all_to_all(right, 'east', split_axis=2, concat_axis=1, tiled=True)  3.23 us
    all_to_all x1, waiting for transfers between devices, local(): lax.all_to_all(left, 'east', split_axis=2, concat_axis=1, tiled=True)  2.86 us
    ppermute x1, starting transfers between devices, local(): lax.ppermute(here_x, 'north', [(to_i, (to_i + 1) % local_part) for to_i i...  1.58 us
    reduce_sum x2, other arithmetic, norm_channels(): centred = values - jnp.mean(values, axis=-1, keepdims=True)  1.19 us
  transfers between devices with their start and end apart: 3, of which 2 were waited for; matrix products, arithmetic and copies ran while one was open for 11% of the time, Pallas kernels for 0%

profile of v1, /device:TPU:0, one launch (start us, length us, event | category | flops | bytes accessed | tf_op | source)
XLA Modules:
  0.0 43.1 jit_solution(13318891484329323369)
XLA Ops:
  0.0 1.1 %convert_reduce_fusion = f32[24,12]{0,1:T(8,128)S(1)} fusion(bf16[24,12,128]{2,0,1:T(8,128)(2,1)} %param.9), kind=kLoop, calls=%fused_computation.29 | loop fusion | flops 73440 | bytes 74880 | tf_op jit(solution)/shard_map/reduce_sum | solution.py:8
  1.3 0.6 %copy-done.4 = f32[128]{0:T(128)S(1)} copy-done((f32[128]{0:T(128)S(1)}, f32[128]{0:T(128)}, u32[]{:S(2)}) %copy-start.4) | copy-done | bytes 536
  2.3 0.6 %copy-done.6 = bf16[128,128]{1,0:T(8,128)(2,1)S(1)} copy-done((bf16[128,128]{1,0:T(8,128)(2,1)S(1)}, bf16[128,128]{1,0:T(8,128)(2,1)}, u32[]{:S(2)}) %copy-start.6) | copy-done | bytes 32792
  3.1 0.4 copy.40
  3.5 1.1 %reshape.41 = bf16[4,2,4608]{2,1,0:T(2,128)(2,1)} reshape(bf16[128,12,24]{2,1,0:T(8,128)(2,1)S(1)} %bitcast.59) | data formatting | bytes 147456
  4.7 6.5 %all-to-all-start = ((bf16[4,2,4608]{2,1,0:T(2,128)(2,1)}), bf16[4,2,4608]{2,1,0:T(2,128)(2,1)S(1)}, u32[]{:S(2)}, u32[]{:S(2)}) async-start(bf16[4,2,4608]{2,1,0:T(2,128)(2,1)} %reshape.41), calls=%async_computation | async-start | bytes 147456 | tf_op jit(solution)/shard_map/all_to_all | solution.py:58
  11.3 0.6 %copy-done.7 = bf16[128,128]{1,0:T(8,128)(2,1)S(1)} copy-done((bf16[128,128]{1,0:T(8,128)(2,1)S(1)}, bf16[128,128]{1,0:T(8,128)(2,1)}, u32[]{:S(2)}) %copy-start.7) | copy-done | bytes 32792
  12.1 0.4 copy.43
  12.5 1.1 %reshape.43 = bf16[4,2,4608]{2,1,0:T(2,128)(2,1)} reshape(bf16[128,12,24]{2,1,0:T(8,128)(2,1)S(1)} %bitcast.60) | data formatting | bytes 147456
  13.7 3.2 %all-to-all-done = bf16[4,2,4608]{2,1,0:T(2,128)(2,1)S(1)} async-done(((bf16[4,2,4608]{2,1,0:T(2,128)(2,1)}), bf16[4,2,4608]{2,1,0:T(2,128)(2,1)S(1)}, u32[]{:S(2)}, u32[]{:S(2)}) %all-to-all-start) | async-done | bytes 73760 | tf_op jit(solution)/shard_map/all_to_all | solution.py:58
  16.9 3.3 %all-to-all-start.1 = ((bf16[4,2,4608]{2,1,0:T(2,128)(2,1)}), bf16[4,2,4608]{2,1,0:T(2,128)(2,1)S(1)}, u32[]{:S(2)}, u32[]{:S(2)}) async-start(bf16[4,2,4608]{2,1,0:T(2,128)(2,1)} %reshape.43), calls=%async_computation.1 | async-start | bytes 147456 | tf_op jit(solution)/shard_map/all_to_all | solution.py:57
  20.2 0.6 %reshape.42 = bf16[128,12,24]{2,1,0:T(8,128)(2,1)S(1)} reshape(bf16[4,2,4608]{2,1,0:T(2,128)(2,1)S(1)} %all-to-all-done) | data formatting | bytes 147456
  20.8 0.4 copy.41
  21.5 1.6 %collective-permute-start = (bf16[24,48,32]{1,0,2:T(8,128)(2,1)S(1)}, bf16[24,48,32]{1,0,2:T(8,128)(2,1)S(1)}, u32[]{:S(2)}, u32[]{:S(2)}) collective-permute-start(bf16[24,48,32]{1,0,2:T(8,128)(2,1)S(1)} %copy.42), channel_id=1, source_target_pairs={{0,4},{4,0},{1,5},{5,1},{2,6},{6,2},{3,7},{7,3},{8,12},{12,8},{9,1... | collective-permute-start | bytes 221192 | tf_op jit(solution)/shard_map/ppermute | solution.py:69
  23.1 2.9 %all-to-all-done.1 = bf16[4,2,4608]{2,1,0:T(2,128)(2,1)S(1)} async-done(((bf16[4,2,4608]{2,1,0:T(2,128)(2,1)}), bf16[4,2,4608]{2,1,0:T(2,128)(2,1)S(1)}, u32[]{:S(2)}, u32[]{:S(2)}) %all-to-all-start.1) | async-done | bytes 73760 | tf_op jit(solution)/shard_map/all_to_all | solution.py:57
  25.9 0.6 %reshape.44 = bf16[128,12,24]{2,1,0:T(8,128)(2,1)S(1)} reshape(bf16[4,2,4608]{2,1,0:T(2,128)(2,1)S(1)} %all-to-all-done.1) | data formatting | bytes 147456
  26.5 0.4 copy.44
  27.7 0.5 %fusion.16 = bf16[24,48,32]{1,0,2:T(8,128)(2,1)S(1)} fusion(s32[]{:T(128)S(6)} %select_n.14, f32[24,24,32]{1,0,2:T(8,128)S(1)} %convolution_bitcast_fusion, f32[24,24,32]{1,0,2:T(8,128)S(1)} %convolution_bitcast_fusion.1), kind=kLoop, calls=%fused_computation.24 | loop fusion | flops 184320 | bytes 221188 | tf_op jit(solution)/shard_map/convert_element_type | solution.py:81
  28.7 10.4 %all_to_all.45 = bf16[4,2,4608]{2,1,0:T(2,128)(2,1)S(1)} all-to-all(bf16[4,2,4608]{2,1,0:T(2,128)(2,1)S(1)} %reshape.45), channel_id=1, replica_groups=mesh['trial'=4,'north'=2,'east'=4] {'east'}, dimensions={0} | all-to-all | bytes 147456 | tf_op jit(solution)/shard_map/all_to_all | solution.py:82
  39.7 0.4 copy.49
  40.4 0.4 copy-done.5
  40.9 0.6 %copy-done.3 = bf16[128,128]{1,0:T(8,128)(2,1)S(1)} copy-done((bf16[128,128]{1,0:T(8,128)(2,1)S(1)}, bf16[128,128]{1,0:T(8,128)(2,1)}, u32[]{:S(2)}) %copy-start.3) | copy-done | bytes 32792
  41.7 0.6 %copy-done.8 = bf16[128,128]{1,0:T(8,128)(2,1)S(1)} copy-done((bf16[128,128]{1,0:T(8,128)(2,1)S(1)}, bf16[128,128]{1,0:T(8,128)(2,1)}, u32[]{:S(2)}) %copy-start.8) | copy-done | bytes 32792
  42.3 0.8 %fusion.12 = bf16[24,12,128]{2,0,1:T(8,128)(2,1)} fusion(f32[24,12,128]{2,0,1:T(8,128)S(1)} %fusion.24, bf16[24,12,128]{2,0,1:T(8,128)(2,1)S(1)} %fusion.22, bf16[128,128]{1,0:T(8,128)(2,1)S(1)} %copy-done.8), kind=kOutput, calls=%fused_computation.17 | convolution fusion | flops 9621504 | bytes 327680 | tf_op jit(solution)/shard_map/ijc,cd->ijd/dot_general | solution.py:34
  (36 shorter events, 3.7 us)
Async XLA Ops:
  0.0 2.1 %copy-start = (bf16[128,128]{1,0:T(8,128)(2,1)S(1)}, bf16[128,128]{1,0:T(8,128)(2,1)}, u32[]{:S(2)}) copy-start(bf16[128,128]{1,0:T(8,128)(2,1)} %param.12) | copy-start | bytes 98308
  0.0 1.1 %copy-start.1 = (bf16[24,12,128]{2,0,1:T(8,128)(2,1)S(1)}, bf16[24,12,128]{2,0,1:T(8,128)(2,1)}, u32[]{:S(2)}) copy-start(bf16[24,12,128]{2,0,1:T(8,128)(2,1)} %param.9) | copy-start | bytes 221188
  1.3 0.7 %copy-start.4 = (f32[128]{0:T(128)S(1)}, f32[128]{0:T(128)}, u32[]{:S(2)}) copy-start(f32[128]{0:T(128)} %param.10) | copy-start | bytes 1540
  2.1 0.8 %copy-start.6 = (bf16[128,128]{1,0:T(8,128)(2,1)S(1)}, bf16[128,128]{1,0:T(8,128)(2,1)}, u32[]{:S(2)}) copy-start(bf16[128,128]{1,0:T(8,128)(2,1)} %param.14) | copy-start | bytes 98308
  4.7 6.5 %copy-start.2 = (bf16[128,128]{1,0:T(8,128)(2,1)S(1)}, bf16[128,128]{1,0:T(8,128)(2,1)}, u32[]{:S(2)}) copy-start(bf16[128,128]{1,0:T(8,128)(2,1)} %param.11) | copy-start | bytes 98308
  4.7 12.2 %all-to-all-start = ((bf16[4,2,4608]{2,1,0:T(2,128)(2,1)}), bf16[4,2,4608]{2,1,0:T(2,128)(2,1)S(1)}, u32[]{:S(2)}, u32[]{:S(2)}) async-start(bf16[4,2,4608]{2,1,0:T(2,128)(2,1)} %reshape.41), calls=%async_computation | async-start | bytes 147456 | tf_op jit(solution)/shard_map/all_to_all | solution.py:58
  11.1 0.8 %copy-start.7 = (bf16[128,128]{1,0:T(8,128)(2,1)S(1)}, bf16[128,128]{1,0:T(8,128)(2,1)}, u32[]{:S(2)}) copy-start(bf16[128,128]{1,0:T(8,128)(2,1)} %param.13) | copy-start | bytes 98308
  16.9 9.0 %all-to-all-start.1 = ((bf16[4,2,4608]{2,1,0:T(2,128)(2,1)}), bf16[4,2,4608]{2,1,0:T(2,128)(2,1)S(1)}, u32[]{:S(2)}, u32[]{:S(2)}) async-start(bf16[4,2,4608]{2,1,0:T(2,128)(2,1)} %reshape.43), calls=%async_computation.1 | async-start | bytes 147456 | tf_op jit(solution)/shard_map/all_to_all | solution.py:57
  21.5 5.9 %collective-permute-start = (bf16[24,48,32]{1,0,2:T(8,128)(2,1)S(1)}, bf16[24,48,32]{1,0,2:T(8,128)(2,1)S(1)}, u32[]{:S(2)}, u32[]{:S(2)}) collective-permute-start(bf16[24,48,32]{1,0,2:T(8,128)(2,1)S(1)} %copy.42), channel_id=1, source_target_pairs={{0,4},{4,0},{1,5},{5,1},{2,6},{6,2},{3,7},{7,3},{8,12},{12,8},{9,1... | collective-permute-start | bytes 221192 | tf_op jit(solution)/shard_map/ppermute | solution.py:69
  40.1 0.7 %copy-start.5 = (f32[128]{0:T(128)S(1)}, f32[128]{0:T(128)}, u32[]{:S(2)}) copy-start(f32[128]{0:T(128)} %param.15) | copy-start | bytes 1540
  40.8 0.8 %copy-start.3 = (bf16[128,128]{1,0:T(8,128)(2,1)S(1)}, bf16[128,128]{1,0:T(8,128)(2,1)}, u32[]{:S(2)}) copy-start(bf16[128,128]{1,0:T(8,128)(2,1)} %param.16) | copy-start | bytes 98308
  41.5 0.8 %copy-start.8 = (bf16[128,128]{1,0:T(8,128)(2,1)S(1)}, bf16[128,128]{1,0:T(8,128)(2,1)}, u32[]{:S(2)}) copy-start(bf16[128,128]{1,0:T(8,128)(2,1)} %param.17) | copy-start | bytes 98308
